TPU v7x, 32 devices: a whole 2x2x4 slice. The times are simulated.
32 devices in a mesh: row: 4 (over z), col: 8 (over y, x, core).
Axes of the slice: x: 2, y: 2, z: 4, core: 2. Of those that a mesh axis runs over, the one named last changes fastest.
Arguments:
- train_points: float32 [4, 32, 4096], P('row', None, 'col'), as said below
- targets: float32 [4, 4096], P('row', 'col'), may hold values from -16 to 16
- inverse_factor: float32 [4, 4096, 1024], P('row', 'col')
- counts: int32 [4, 4], P('row'), may hold values from 512 to 1024, as said below
- membership: int32 [4, 4, 16], replicated, may hold values from 0 to 1, as said below
- test_points: float32 [16, 32, 128], P('row'), may hold values from -6 to 6
Outputs:
- pred_mean: float32 [16, 128], P('row')
- pred_var: float32 [16, 128], P('row')
Inputs may be any that keep to these rules, and one draw needn't show every extreme that they name: Each expert membership[r, c, :] takes part in at least one and at most 4 blocks, exactly 4 for at least one expert, and in at most one of the 4 blocks of each owner row. `counts`: at least one expert has all 1024 points valid. `train_points`: each expert's 1024 points are drawn independently of the other experts' points.
All inputs are finite; a program needn't handle non-finite values.
Results may differ from a plain program's by a relative error of at most 0.0003.
Values sent between devices are 32-bit elements; how exact they have to be, the bound alone decides.
A program may use at most 64 MiB of HBM per device.

v0:
```python
import functools

import jax
import jax.numpy as jnp
from jax import lax
from jax.experimental import pallas as pl
from jax.experimental.pallas import tpu as pltpu
from jax.sharding import PartitionSpec as P

SIGNAL = 1.0
NOISE = 0.1
F32 = jnp.float32
BF16 = jnp.bfloat16
MESH = pl.DeviceIdType.MESH


def high_low(value):
    high = value.astype(BF16)
    return high, (value - high.astype(F32)).astype(BF16)


def expert_kernel(
    rows, cols,
    counts_hbm, member_hbm, train_ref, target_ref, factor_ref, test_ref,
    sums_ref,
    factor_buf, own_x, own_y, tests, other_x, other_y, sent_tests, got_tests,
    factor_high, factor_low, nat_a, nat_b, points, k_high, k_low,
    sent_parts, got_parts, taken_by, sent_bytes, alpha, counts_ref, member_ref,
    local_sems, x_send, x_recv, t_send, t_recv, p_send, p_recv,
):
    row = lax.axis_index("row")
    col = lax.axis_index("col")
    parity = col % 2
    expert = col // 2
    experts = cols // 2
    blocks, features, length = tests.shape
    half = own_x.shape[1]
    partner = (row, expert * 2 + 1 - parity)

    others = [lax.rem(row + d, rows) for d in range(1, rows)]
    mates = [lax.rem(expert + d, experts) for d in range(1, experts)]
    barrier = pltpu.get_barrier_semaphore()
    peers = [partner]
    for r in others:
        peers += [(r, expert * 2), (r, expert * 2 + 1)]
    for c in mates:
        peers += [(row, c * 2), (row, c * 2 + 1)]
    for peer in peers:
        pl.semaphore_signal(barrier, inc=1, device_id=peer, device_id_type=MESH)

    load_member = pltpu.make_async_copy(member_hbm, member_ref, local_sems.at[4])
    load_counts = pltpu.make_async_copy(counts_hbm, counts_ref, local_sems.at[5])
    load_tests = pltpu.make_async_copy(test_ref, tests, local_sems.at[0])
    load_member.start()
    load_x = pltpu.make_async_copy(train_ref.at[0], own_x, local_sems.at[1])
    load_y = pltpu.make_async_copy(target_ref, own_y, local_sems.at[2])
    load_f = pltpu.make_async_copy(factor_ref.at[0], factor_buf, local_sems.at[3])
    load_tests.start()
    load_x.start()
    load_y.start()
    load_counts.start()
    load_f.start()

    def chosen_in(row_at, owner):
        at = jnp.int32(0)
        for j in range(1, blocks):
            at = at + j * member_ref[row_at, expert, owner * blocks + j]
        return at

    load_member.wait()
    load_tests.wait()
    for d, r in enumerate(others):
        sent_tests[d] = tests[chosen_in(r, row)]
    pl.semaphore_wait(barrier, len(peers))

    def remote(src, dst, send, recv, peer):
        copy = pltpu.make_async_remote_copy(
            src_ref=src, dst_ref=dst, send_sem=send, recv_sem=recv,
            device_id=peer, device_id_type=MESH,
        )
        copy.start()
        return copy

    load_x.wait()
    load_y.wait()
    x_copy = remote(own_x, other_x, x_send.at[0], x_recv.at[0], partner)
    y_copy = remote(own_y, other_y, x_send.at[1], x_recv.at[1], partner)
    test_copies = [
        remote(sent_tests.at[d], got_tests.at[d], t_send.at[d], t_recv.at[d],
               (r, col))
        for d, r in enumerate(others)
    ]

    def stacked(x, y):
        xh = x.astype(BF16).astype(F32)
        xl = x - xh
        x2 = jnp.sum(x * x, axis=0, keepdims=True)
        a = x2.astype(BF16).astype(F32)
        b = (x2 - a).astype(BF16).astype(F32)
        c = x2 - a - b
        yh = y.astype(BF16).astype(F32)
        yl = y - yh
        at = lax.broadcasted_iota(jnp.int32, (8, half), 0)
        tail = jnp.zeros((8, half), F32)
        for i, v in enumerate((a, b, c, yh, yl)):
            tail = jnp.where(at == i, v, tail)
        first = jnp.concatenate([xh, xl, xh, xl], axis=0)
        last = jnp.concatenate([tail, jnp.zeros((120, half), F32)], axis=0)
        return first.T, last.T

    def put(a, b, offset):
        nat_a[pl.ds(offset, half, stride=2), :] = a
        nat_b[pl.ds(offset, half, stride=2), :] = b

    a, b = stacked(own_x[...], own_y[...])

    @pl.when(parity == 0)
    def _():
        put(a, b, 0)

    @pl.when(parity == 1)
    def _():
        put(a, b, 1)

    load_f.wait()
    fh, fl = high_low(factor_buf[...])
    factor_high[...] = fh
    factor_low[...] = fl

    x_copy.wait_recv()
    y_copy.wait_recv()
    a2, b2 = stacked(other_x[...], other_y[...])

    @pl.when(parity == 1)
    def _():
        put(a2, b2, 0)

    @pl.when(parity == 0)
    def _():
        put(a2, b2, 1)

    points[:, :128] = nat_a[...].astype(BF16)
    points[:, 128:] = nat_b[...].astype(BF16)
    solved_y = jnp.dot(factor_high[...], points[:, 128:], preferred_element_type=F32)
    solved_y += jnp.dot(factor_low[...], points[:, 128:], preferred_element_type=F32)
    whitened = solved_y[:, 3:4] + solved_y[:, 4:5]
    solved_back = jnp.sum(factor_buf[...] * whitened, axis=0, keepdims=True)
    for i in range(0, 2 * half, 128):
        alpha[i:i + 128, :] = jnp.broadcast_to(solved_back[:, i:i + 128], (128, 128)).T

    load_counts.wait()
    valid = counts_ref[0, expert]
    pair = 2 * length
    tail_at = lax.broadcasted_iota(jnp.int32, (128, pair), 0)
    tail_t = jnp.where(tail_at < 3, -1.0, 0.0).astype(BF16)
    chunk = 128
    order = [None] + list(range(rows - 1))
    owners = [row] + [lax.rem(row + rows - d - 1, rows) for d in range(rows - 1)]
    for first in range(0, rows, 2):
        taken = []
        for s in (first, first + 1):
            d = order[s]
            if d is None:
                taken.append(tests[chosen_in(row, row)])
            else:
                test_copies[d].wait_recv()
                taken.append(got_tests[d])
        t = jnp.concatenate(taken, axis=1)
        th, tl = high_low(2.0 * t)
        t2 = jnp.sum(t * t, axis=0, keepdims=True)
        rhs = jnp.concatenate([th, th, tl, tl, tail_t], axis=0)
        mean = jnp.zeros((1, pair), F32)
        for i in range(0, 2 * half, chunk):
            e = jnp.dot(points[i:i + chunk, :], rhs, preferred_element_type=F32) - t2
            k = jnp.exp(e * (1.0 / features))
            at = lax.broadcasted_iota(jnp.int32, (chunk, pair), 0) + i
            k = jnp.where(at < valid, SIGNAL * k, 0.0)
            along = alpha[i:i + chunk, :]
            mean += jnp.sum(k * jnp.concatenate([along, along], axis=1), axis=0, keepdims=True)
            kh, kl = high_low(k)
            k_high[i:i + chunk, :] = kh
            k_low[i:i + chunk, :] = kl
        solved = jnp.dot(factor_high[...], k_high[...], preferred_element_type=F32)
        solved += jnp.dot(factor_low[...], k_high[...], preferred_element_type=F32)
        solved += jnp.dot(factor_high[...], k_low[...], preferred_element_type=F32)
        quad = jnp.sum(solved * solved, axis=0, keepdims=True)
        for n, s in enumerate((first, first + 1)):
            lanes = slice(n * length, (n + 1) * length)
            d = order[s]
            sent_parts[s, 0:1, :] = mean[:, lanes]
            sent_parts[s, 1:2, :] = quad[:, lanes]
            mine = got_parts.at[expert, parity, row]
            if d is None:
                keep = pltpu.make_async_copy(sent_parts.at[s], mine, p_recv.at[0])
                keep.start()
                targets = [partner]
                for c in mates:
                    targets += [(row, c * 2), (row, c * 2 + 1)]
            else:
                targets = [(owners[s], lax.rem(col + c, cols)) for c in range(cols)]
            for target in targets:
                remote(sent_parts.at[s], mine, p_send.at[s], p_recv.at[0], target)

    for j in range(blocks):
        for e in range(experts):
            for r in range(rows):
                on = member_ref[r, e, row * blocks + j]
                n = e * rows + r
                taken_by[j, n:n + 1, :] = jnp.full((1, length), on, jnp.int32).astype(F32)

    pltpu.make_async_copy(got_parts, got_parts, p_recv.at[0]).wait()
    total = got_parts[:, 0] + got_parts[:, 1]
    total = total.reshape(experts * rows, 2, length)
    mean = total[:, 0, :]
    quad = total[:, 1, :]
    variance = NOISE + jnp.maximum(SIGNAL - quad, 0.0)
    gap = 0.5 * (jnp.log(jnp.full_like(variance, SIGNAL + NOISE)) - jnp.log(variance))
    weight = gap / variance
    weighted = weight * mean
    for j in range(blocks):
        on = taken_by[j] > 0.5
        sums_ref[j:j + 1, :] = jnp.sum(jnp.where(on, weighted, 0.0), axis=0, keepdims=True)
        sums_ref[blocks + j:blocks + j + 1, :] = jnp.sum(
            jnp.where(on, weight, 0.0), axis=0, keepdims=True)
    x_copy.wait_send()
    y_copy.wait_send()
    for copy in test_copies:
        copy.wait_send()
    for s in range(rows):
        sent = cols - 1 if order[s] is None else cols
        flat = sent_bytes.at[pl.ds(0, sent)]
        pltpu.make_async_copy(flat, flat, p_send.at[s]).wait()


def on_device(rows, cols, train_points, targets, inverse_factor, counts, membership, test_points):
    features, half = train_points.shape[1:]
    blocks, _, length = test_points.shape
    points = inverse_factor.shape[2]
    experts = cols // 2
    vmem, dma = pltpu.VMEM, pltpu.SemaphoreType.DMA
    anywhere = pl.BlockSpec(memory_space=pltpu.HBM)
    sums = pl.pallas_call(
        functools.partial(expert_kernel, rows, cols),
        out_shape=jax.ShapeDtypeStruct((2 * blocks, length), F32),
        in_specs=[anywhere] * 6,
        out_specs=pl.BlockSpec(memory_space=pltpu.VMEM),
        scratch_shapes=[
            vmem((half, points), F32),
            vmem((features, half), F32),
            vmem((1, half), F32),
            vmem((blocks, features, length), F32),
            vmem((features, half), F32),
            vmem((1, half), F32),
            vmem((rows - 1, features, length), F32),
            vmem((rows - 1, features, length), F32),
            vmem((half, points), BF16),
            vmem((half, points), BF16),
            vmem((points, 128), F32),
            vmem((points, 128), F32),
            vmem((points, 256), BF16),
            vmem((points, 2 * length), BF16),
            vmem((points, 2 * length), BF16),
            vmem((rows, 2, length), F32),
            vmem((experts, 2, rows, 2, length), F32),
            vmem((blocks, experts * rows, length), F32),
            vmem((cols, 2, length), F32),
            vmem((points, 128), F32),
            pltpu.SMEM(counts.shape, jnp.int32),
            pltpu.SMEM(membership.shape, jnp.int32),
            dma((6,)),
            dma((2,)),
            dma((2,)),
            dma((rows - 1,)),
            dma((rows - 1,)),
            dma((rows,)),
            dma((1,)),
        ],
        compiler_params=pltpu.CompilerParams(
            collective_id=0, has_side_effects=True
        ),
    )(counts, membership, train_points, targets, inverse_factor, test_points)
    precision_sum = 1.0 / (SIGNAL + NOISE) + sums[blocks:]
    return (sums[:blocks] / precision_sum, 1.0 / precision_sum)


def solution(mesh):
    in_specs = (
        P("row", None, "col"),
        P("row", "col"),
        P("row", "col", None),
        P("row", None),
        P(),
        P("row", None, None),
    )
    out_specs = (P("row", None), P("row", None))
    body = functools.partial(on_device, mesh.shape["row"], mesh.shape["col"])
    return jax.shard_map(
        body, mesh=mesh, in_specs=in_specs, out_specs=out_specs, check_vma=False
    )
```

profile of v0, /device:TPU:0, one launch (start us, length us, event | category | flops | bytes accessed | tf_op | source)
XLA Modules:
  0.0 19.5 jit_solution(16294942082509077467)
XLA Ops:
  0.6 17.5 %shard_map.77 = f32[8,128]{1,0:T(8,128)} custom-call(s32[1,4]{1,0:T(1,128)} %counts_hbm.1, s32[4,4,16]{2,1,0:T(4,128)} %member_hbm.1, f32[1,32,512]{2,1,0:T(8,128)} %train_ref.1, f32[1,512]{1,0:T(1,128)} %target_ref.1, f32[1,512,1024]{2,1,0:T(8,128)} %factor_ref.1, f32[4,32,128]{2,1,0:T(8,128)} %test_ref.1), custom_call_target="tpu_custom_call" | custom-call | tf_op jit(solution)/shard_map/pallas_call | solution.py:242
  18.2 1.3 %fusion = (f32[4,128]{1,0:T(4,128)}, f32[4,128]{1,0:T(4,128)}) fusion(f32[8,128]{1,0:T(8,128)} %shard_map.77), kind=kLoop, calls=%fused_computation.2 | loop fusion | flops 1536 | bytes 8192 | tf_op jit(solution)/shard_map/div | solution.py:283
where the time goes:
time: 19.8 us; the launch traced here: 19.5 us
  Pallas kernels  17.5 us (88%)
  other arithmetic  1.34 us (7%)
  between operations  0.64 us (3%)
    pallas_call x1, Pallas kernels, on_device(): pl.pallas_call(functools.partial(expert_kernel, rows, cols), out_shape=ja...  17.5 us
    div x1, other arithmetic, on_device(): return (sums[:blocks] / precision_sum, 1.0 / precision_sum)  1.34 us

commit v1 on v0

v1 whole, which is shorter than its diff:
```python
import functools
import math

import jax
import jax.numpy as jnp
from jax import lax
from jax.experimental import pallas as pl
from jax.experimental.pallas import tpu as pltpu
from jax.sharding import PartitionSpec as P

SIGNAL = 1.0
NOISE = 0.1
F32 = jnp.float32
BF16 = jnp.bfloat16
MESH = pl.DeviceIdType.MESH
LANES = 128
FAR = 2.0 ** 15


def high_low(value):
    high = value.astype(BF16)
    return high, (value - high.astype(F32)).astype(BF16)


def three_parts(value):
    a = value.astype(BF16).astype(F32)
    b = (value - a).astype(BF16).astype(F32)
    return a, b, value - a - b


def in_rows(parts, width):
    at = lax.broadcasted_iota(jnp.int32, (8, width), 0)
    tail = jnp.zeros((8, width), F32)
    for i, v in parts:
        tail = jnp.where(at == i, v, tail)
    return tail


def folded(value):
    rows, width = value.shape
    return jnp.sum(value.reshape(rows // 8, 8, width), axis=0)


def expert_kernel(
    rows, cols,
    counts_hbm, member_hbm, train_ref, target_ref, factor_ref, test_ref,
    sums_ref,
    factor_buf, own_x, own_y, tests, other_x, other_y, sent_tests, got_tests,
    stack, nat_a, nat_b, points, k_cat, white,
    sent_parts, got_parts, taken_by, sent_bytes, counts_ref, member_ref,
    local_sems, factor_sems, x_send, x_recv, t_send, t_recv, p_send, p_recv,
):
    row = lax.axis_index("row")
    col = lax.axis_index("col")
    parity = col % 2
    expert = col // 2
    experts = cols // 2
    blocks, features, length = tests.shape
    half = own_x.shape[1]
    tall = 2 * LANES
    steps = half // LANES
    partner = (row, expert * 2 + 1 - parity)

    others = [lax.rem(row + d, rows) for d in range(1, rows)]
    mates = [lax.rem(expert + d, experts) for d in range(1, experts)]
    barrier = pltpu.get_barrier_semaphore()
    peers = [partner]
    for r in others:
        peers += [(r, expert * 2), (r, expert * 2 + 1)]
    for c in mates:
        peers += [(row, c * 2), (row, c * 2 + 1)]
    for peer in peers:
        pl.semaphore_signal(barrier, inc=1, device_id=peer, device_id_type=MESH)

    load_member = pltpu.make_async_copy(member_hbm, member_ref, local_sems.at[4])
    load_counts = pltpu.make_async_copy(counts_hbm, counts_ref, local_sems.at[5])
    load_tests = pltpu.make_async_copy(test_ref, tests, local_sems.at[0])
    load_x = pltpu.make_async_copy(train_ref.at[0], own_x, local_sems.at[1])
    load_y = pltpu.make_async_copy(target_ref, own_y, local_sems.at[2])
    load_member.start()
    load_tests.start()
    load_x.start()
    load_y.start()
    load_counts.start()
    loads = []
    for b in range(steps):
        part = (pl.ds(b * LANES, LANES), pl.ds(0, tall * (b + 1)))
        loads.append(pltpu.make_async_copy(
            factor_ref.at[0].at[part], factor_buf.at[part], factor_sems.at[b]))
        loads[b].start()

    def chosen_in(row_at, owner):
        at = jnp.int32(0)
        for j in range(1, blocks):
            at = at + j * member_ref[row_at, expert, owner * blocks + j]
        return at

    load_member.wait()
    load_tests.wait()
    for d, r in enumerate(others):
        sent_tests[d] = tests[chosen_in(r, row)]
    load_x.wait()
    load_y.wait()
    pl.semaphore_wait(barrier, len(peers))

    def remote(src, dst, send, recv, peer):
        copy = pltpu.make_async_remote_copy(
            src_ref=src, dst_ref=dst, send_sem=send, recv_sem=recv,
            device_id=peer, device_id_type=MESH,
        )
        copy.start()
        return copy

    test_copies = [
        remote(sent_tests.at[d], got_tests.at[d], t_send.at[d], t_recv.at[d],
               (r, col))
        for d, r in enumerate(others)
    ]
    x_copy = remote(own_x, other_x, x_send.at[0], x_recv.at[0], partner)
    y_copy = remote(own_y, other_y, x_send.at[1], x_recv.at[1], partner)

    load_counts.wait()
    valid = counts_ref[0, expert]
    scale = math.log2(math.e) / features

    def stacked(x, y, offset):
        at = 2 * lax.broadcasted_iota(jnp.int32, (1, half), 1) + offset
        inside = at < valid
        x = jnp.where(inside, x, 0.0)
        xh = x.astype(BF16).astype(F32)
        xl = x - xh
        a, b, c = three_parts(scale * jnp.sum(x * x, axis=0, keepdims=True))
        a = jnp.where(inside, a, FAR)
        yh = y.astype(BF16).astype(F32)
        one = jnp.ones((1, half), F32)
        tail = in_rows(
            enumerate((a, b, c, yh, y - yh, one, one, one)), half)
        first = jnp.concatenate([xh, xl, xh, xl], axis=0)
        last = jnp.concatenate([tail, jnp.zeros((LANES - 8, half), F32)], axis=0)
        return first.T, last.T

    def put(a, b, offset):
        nat_a[pl.ds(offset, half, stride=2), :] = a
        nat_b[pl.ds(offset, half, stride=2), :] = b

    a, b = stacked(own_x[...], own_y[...], parity)

    @pl.when(parity == 0)
    def _():
        put(a, b, 0)

    @pl.when(parity == 1)
    def _():
        put(a, b, 1)

    for b in range(steps):
        loads[b].wait()
        width = tall * (b + 1)
        fh, fl = high_low(factor_buf[b * LANES:(b + 1) * LANES, :width])
        stack[b * tall:b * tall + LANES, :width] = fh
        stack[b * tall + LANES:(b + 1) * tall, :width] = fl

    x_copy.wait_recv()
    y_copy.wait_recv()
    a2, b2 = stacked(other_x[...], other_y[...], 1 - parity)

    @pl.when(parity == 1)
    def _():
        put(a2, b2, 0)

    @pl.when(parity == 0)
    def _():
        put(a2, b2, 1)

    points[:, :LANES] = nat_a[...].astype(BF16)
    points[:, LANES:] = nat_b[...].astype(BF16)
    for b in range(steps):
        width = tall * (b + 1)
        out = jnp.dot(stack[b * tall:(b + 1) * tall, :width],
                      points[:width, LANES:], preferred_element_type=F32)
        both = out[:LANES] + out[LANES:]
        line = both[:, 3:4] + both[:, 4:5]
        white[b * LANES:(b + 1) * LANES, :] = jnp.broadcast_to(line, (LANES, length))

    order = [None] + list(range(rows - 1))
    owners = [row] + [lax.rem(row + rows - d - 1, rows) for d in range(rows - 1)]
    for s in range(rows):
        d = order[s]
        if d is None:
            t = tests[chosen_in(row, row)]
        else:
            test_copies[d].wait_recv()
            t = got_tests[d]
        th, tl = high_low((2.0 * scale) * t)
        t2 = three_parts(-scale * jnp.sum(t * t, axis=0, keepdims=True))
        minus = jnp.full((1, length), -1.0, F32)
        tail = in_rows([*enumerate((minus,) * 3), *enumerate(t2, 5)], length)
        last = jnp.concatenate(
            [tail, jnp.zeros((LANES - 8, length), F32)], axis=0).astype(BF16)
        rhs = jnp.concatenate([th, th, tl, tl, last], axis=0)
        mean = jnp.zeros((8, length), F32)
        quad = jnp.zeros((8, length), F32)
        for b in range(steps):
            at = slice(b * tall, (b + 1) * tall)
            k = SIGNAL * jnp.exp2(
                jnp.dot(points[at, :], rhs, preferred_element_type=F32))
            kh, kl = high_low(k)
            k_cat[at, :length] = kh
            k_cat[at, length:] = kl
        for b in range(steps):
            at = slice(b * tall, (b + 1) * tall)
            out = jnp.dot(stack[at, :tall * (b + 1)], k_cat[:tall * (b + 1), :],
                          preferred_element_type=F32)
            both = out[:LANES] + out[LANES:]
            solved = both[:, :length] + both[:, length:]
            quad += folded(solved * solved)
            mean += folded(solved * white[b * LANES:(b + 1) * LANES, :])
        sent_parts[s, 0:1, :] = jnp.sum(mean, axis=0, keepdims=True)
        sent_parts[s, 1:2, :] = jnp.sum(quad, axis=0, keepdims=True)
        mine = got_parts.at[expert, parity, row]
        if d is None:
            keep = pltpu.make_async_copy(sent_parts.at[s], mine, p_recv.at[0])
            keep.start()
            targets = [partner]
            for c in mates:
                targets += [(row, c * 2), (row, c * 2 + 1)]
        else:
            targets = [(owners[s], lax.rem(col + c, cols)) for c in range(cols)]
        for target in targets:
            remote(sent_parts.at[s], mine, p_send.at[s], p_recv.at[0], target)

    for j in range(blocks):
        for e in range(experts):
            for r in range(rows):
                on = member_ref[r, e, row * blocks + j]
                n = e * rows + r
                taken_by[j, n:n + 1, :] = jnp.full((1, length), on, jnp.int32).astype(F32)

    pltpu.make_async_copy(got_parts, got_parts, p_recv.at[0]).wait()
    total = got_parts[:, 0] + got_parts[:, 1]
    total = total.reshape(experts * rows, 2, length)
    mean = total[:, 0, :]
    quad = total[:, 1, :]
    variance = NOISE + jnp.maximum(SIGNAL - quad, 0.0)
    gap = 0.5 * (jnp.log(jnp.full_like(variance, SIGNAL + NOISE)) - jnp.log(variance))
    weight = gap / variance
    weighted = weight * mean
    for j in range(blocks):
        on = taken_by[j] > 0.5
        sums_ref[j:j + 1, :] = jnp.sum(jnp.where(on, weighted, 0.0), axis=0, keepdims=True)
        sums_ref[blocks + j:blocks + j + 1, :] = jnp.sum(
            jnp.where(on, weight, 0.0), axis=0, keepdims=True)
    x_copy.wait_send()
    y_copy.wait_send()
    for copy in test_copies:
        copy.wait_send()
    for s in range(rows):
        sent = cols - 1 if order[s] is None else cols
        flat = sent_bytes.at[pl.ds(0, sent)]
        pltpu.make_async_copy(flat, flat, p_send.at[s]).wait()


def on_device(rows, cols, train_points, targets, inverse_factor, counts, membership, test_points):
    features, half = train_points.shape[1:]
    blocks, _, length = test_points.shape
    points = inverse_factor.shape[2]
    experts = cols // 2
    vmem, dma = pltpu.VMEM, pltpu.SemaphoreType.DMA
    anywhere = pl.BlockSpec(memory_space=pltpu.HBM)
    sums = pl.pallas_call(
        functools.partial(expert_kernel, rows, cols),
        out_shape=pltpu.VMEM((2 * blocks, length), F32),
        in_specs=[anywhere] * 6,
        out_specs=pl.BlockSpec(memory_space=pltpu.VMEM),
        scratch_shapes=[
            vmem((half, points), F32),
            vmem((features, half), F32),
            vmem((1, half), F32),
            vmem((blocks, features, length), F32),
            vmem((features, half), F32),
            vmem((1, half), F32),
            vmem((rows - 1, features, length), F32),
            vmem((rows - 1, features, length), F32),
            vmem((2 * half, points), BF16),
            vmem((points, LANES), F32),
            vmem((points, LANES), F32),
            vmem((points, 2 * LANES), BF16),
            vmem((points, 2 * length), BF16),
            vmem((half, length), F32),
            vmem((rows, 2, length), F32),
            vmem((experts, 2, rows, 2, length), F32),
            vmem((blocks, experts * rows, length), F32),
            vmem((cols, 2, length), F32),
            pltpu.SMEM(counts.shape, jnp.int32),
            pltpu.SMEM(membership.shape, jnp.int32),
            dma((6,)),
            dma((half // LANES,)),
            dma((2,)),
            dma((2,)),
            dma((rows - 1,)),
            dma((rows - 1,)),
            dma((rows,)),
            dma((1,)),
        ],
        compiler_params=pltpu.CompilerParams(
            collective_id=0, has_side_effects=True
        ),
    )(counts, membership, train_points, targets, inverse_factor, test_points)
    precision_sum = 1.0 / (SIGNAL + NOISE) + sums[blocks:]
    return (sums[:blocks] / precision_sum, 1.0 / precision_sum)


def solution(mesh):
    in_specs = (
        P("row", None, "col"),
        P("row", "col"),
        P("row", "col", None),
        P("row", None),
        P(),
        P("row", None, None),
    )
    out_specs = (P("row", None), P("row", None))
    body = functools.partial(on_device, mesh.shape["row"], mesh.shape["col"])
    return jax.shard_map(
        body, mesh=mesh, in_specs=in_specs, out_specs=out_specs, check_vma=False
    )
```

time: 19.8 us -> 17 us (0.86)
  Pallas kernels: 17.5 us -> 15.5 us
  other arithmetic: 1.34 us -> 0.59 us
    pallas_call x1, Pallas kernels: 17.5 us -> 15.5 us  [on_device(): pl.pallas_call(functools.partial(expert_kernel, rows, cols), out_shape=pl...]
    div x1, other arithmetic: 1.34 us -> 0.59 us  [on_device(): return (sums[:blocks] / precision_sum, 1.0 / precision_sum)]
where the time goes in v1:
time: 17 us; the launch traced here: 16.8 us
  Pallas kernels  15.5 us (91%)
  between operations  0.64 us (4%)
  other arithmetic  0.59 us (3%)
    pallas_call x1, Pallas kernels, on_device(): pl.pallas_call(functools.partial(expert_kernel, rows, cols), out_shape=pl...  15.5 us
    div x1, other arithmetic, on_device(): return (sums[:blocks] / precision_sum, 1.0 / precision_sum)  0.59 us

profile of v1, /device:TPU:0, one launch (start us, length us, event | category | flops | bytes accessed | tf_op | source)
XLA Modules:
  0.0 16.8 jit_solution(17632756313425978743)
XLA Ops:
  0.6 15.5 %shard_map.77 = f32[8,128]{1,0:T(8,128)S(1)} custom-call(s32[1,4]{1,0:T(1,128)} %counts_hbm.1, s32[4,4,16]{2,1,0:T(4,128)} %member_hbm.1, f32[1,32,512]{2,1,0:T(8,128)} %train_ref.1, f32[1,512]{1,0:T(1,128)} %target_ref.1, f32[1,512,1024]{2,1,0:T(8,128)} %factor_ref.1, f32[4,32,128]{2,1,0:T(8,128)} %test_ref.1), custom_call_target="tpu_custom_call" | custom-call | tf_op jit(solution)/shard_map/pallas_call | solution.py:270
  16.2 0.6 %fusion = (f32[4,128]{1,0:T(4,128)}, f32[4,128]{1,0:T(4,128)}) fusion(f32[8,128]{1,0:T(8,128)S(1)} %shard_map.77), kind=kLoop, calls=%fused_computation.2 | loop fusion | flops 1536 | bytes 8192 | tf_op jit(solution)/shard_map/div | solution.py:310
